TPU v7x, 256 devices: a whole 4x4x8 slice. The times are simulated.
256 devices in a mesh: node: 256 (over z, x, y, core).
Axes of the slice: x: 4, y: 4, z: 8, core: 2. Of those that a mesh axis runs over, the one named last changes fastest.
Arguments:
- round_index: int32 [1], replicated, may hold values from 0 to 63
- sample_ids: int32 [256, 8], P('node'), may hold values from 0 to 3
- token_pool: bfloat16 [256, 4, 64, 512], P('node'), may hold values from -20 to 20
- cotangent_pool: bfloat16 [256, 4, 64, 512], P('node'), may hold values from -6 to 6
- weights: bfloat16 [256, 4, 512, 512], P('node'), may hold values from -12 to 12
- residue: bfloat16 [256, 4, 512, 512], P('node'), may hold values from -6 to 6
Outputs:
- new_weights: bfloat16 [256, 4, 512, 512], P('node')
- new_residue: bfloat16 [256, 4, 512, 512], P('node')
- grad_rms: float32 [], replicated
All inputs are finite; a program needn't handle non-finite values.
Results may differ from a plain program's by a relative error of at most 0.0065.
Values may be sent and summed in bfloat16 or wider, within the bound.
No kernel may reach another device: no remote copies, remote signals or barrier semaphores. Data moves between devices by JAX's collectives and lax.ppermute only.
A program may use at most 128 MiB of HBM per device.

v0:
```python
from functools import partial

import jax
import jax.numpy as jnp
from jax import lax
from jax.experimental import pallas as pl
from jax.experimental.pallas import tpu as pltpu
from jax.sharding import Mesh
from jax.sharding import PartitionSpec as P

NODE = ("z", "x", "y", "core")
SIZES = (8, 4, 4, 2)
LEVELS = 8
CUT = 1568
step_rate = 0.1

epsilon = 1e-06
PARTS = (2048,)
bf16, f32 = jnp.bfloat16, jnp.float32


def dot(a, b, ca, cb):
    return lax.dot_general(a, b, (((ca,), (cb,)), ((), ())), preferred_element_type=f32)


def gradient_kernel(looped, ids, tok, cot, w, res, out0, sq, wbuf, rbuf, tbuf, tokb, cotb, proj, grads, sem_in, sem_r, sem_out):
    images, seq, width = tok.shape
    rows = images * seq
    group, head = 256, 64
    outs = (out0,)
    scale = width**-0.5
    loads = [pltpu.make_async_copy(tok, tokb, sem_in.at[0]), pltpu.make_async_copy(cot, cotb, sem_in.at[1])]
    wloads = [pltpu.make_async_copy(w.at[m], wbuf.at[m], sem_in.at[2 + m]) for m in range(4)]
    rloads = [pltpu.make_async_copy(res.at[m], rbuf.at[m], sem_r.at[m]) for m in range(4)]
    pieces, row = [], 0
    for out in outs:
        start, end = row, row + out.shape[0]
        while row < end:
            m, at = divmod(row, width)
            size = min(end - row, width - at)
            pieces.append((pl.ds(at, size), out.at[pl.ds(row - start, size)], m))
            row += size
    stores = [pltpu.make_async_copy(tbuf.at[m, r], o, sem_out.at[j]) for j, (r, o, m) in enumerate(pieces)]
    for c in (loads[0], wloads[0], wloads[1], loads[1], wloads[3], wloads[2], *rloads):
        c.start()

    count = [jnp.int32(0)] * images
    for j in range(ids.shape[0]):
        for b in range(images):
            count[b] = count[b] + (ids[j] == b).astype(jnp.int32)
    count = [c.astype(f32) for c in count]

    loads[0].wait()
    values = tokb[...].reshape(rows, width).astype(f32)
    centered = values - jnp.mean(values, -1, keepdims=True)
    variance = jnp.mean(centered * centered, -1, keepdims=True)
    normed = (centered * lax.rsqrt(variance + epsilon)).astype(bf16)
    for m, extra in ((0, head**-0.5), (1, 1.0), (2, 1.0)):
        wloads[m].wait()
        proj[m] = (dot(normed, wbuf[m], 1, 0) * scale).astype(bf16) * bf16(extra)
    loads[1].wait()
    wloads[3].wait()
    grad_rows = cotb[...].reshape(rows, width)
    proj[3] = (dot(grad_rows, wbuf[3], 1, 1) * scale).astype(bf16)

    heads = group // head
    same = (
        lax.broadcasted_iota(jnp.int32, (heads * seq, group), 0) // seq
        == lax.broadcasted_iota(jnp.int32, (heads * seq, group), 1) // head
    )
    own = same.astype(f32).astype(bf16)
    lane_head = lax.broadcasted_iota(jnp.int32, (seq, group), 1) // head

    def diagonal(x):
        out = x[:seq]
        for h in range(1, heads):
            out = jnp.where(lane_head == h, x[h * seq : (h + 1) * seq], out)
        return out

    def attend(b, share):
        r = pl.ds(b * seq if isinstance(b, int) else pl.multiple_of(b * seq, seq), seq)
        for g in range(width // group):
            c = slice(g * group, (g + 1) * group)
            q, k, v, d = (proj[m, r, c] for m in range(4))
            qs = jnp.concatenate([q] * heads, 0) * own
            ds = jnp.concatenate([d] * heads, 0) * own
            s = dot(k, qs, 1, 1)
            e = jnp.exp(s - jnp.max(s, 0, keepdims=True))
            p = e * (1.0 / jnp.sum(e, 0, keepdims=True))
            ph = p.astype(bf16)
            dp = dot(v, ds, 1, 1)
            sg = (p * (dp - jnp.sum(dp * p, 0, keepdims=True)) * share).astype(bf16)
            grads[2, r, c] = (dot(ph, ds, 1, 0) * share).astype(bf16)
            grads[1, r, c] = dot(sg, qs, 1, 0).astype(bf16)
            grads[3, r, c] = (diagonal(dot(ph, v, 0, 0)) * share).astype(bf16)
            grads[0, r, c] = (diagonal(dot(sg, k, 0, 0)) * head**-0.5).astype(bf16)

    if looped:

        @pl.loop(0, images)
        def _(b):
            share = jnp.int32(0)
            for j in range(ids.shape[0]):
                share = share + (ids[j] == b).astype(jnp.int32)
            attend(b, share.astype(f32))

    else:
        for b in range(images):
            attend(b, count[b])

    total = jnp.zeros((8, width), f32)
    for m in range(4):
        left, right = (grads[3], grad_rows) if m == 3 else (normed, grads[m])
        gradient = dot(left, right, 0, 0) * scale
        rloads[m].wait()
        tbuf[m] = (rbuf[m].astype(f32) + gradient).astype(bf16)
        for store, piece in zip(stores, pieces):
            if piece[2] == m:
                store.start()
        total = total + jnp.sum((gradient * gradient).reshape(-1, 8, width), 0)
    sq[0] = jnp.sum(total)
    for store in stores:
        store.wait()


def gradient_call(ids, tok, cot, w, res, looped=False):
    images, seq, width = tok.shape
    rows = images * seq
    hbm = pl.BlockSpec(memory_space=pl.ANY)
    smem = pl.BlockSpec(memory_space=pltpu.SMEM)
    return pl.pallas_call(
        partial(gradient_kernel, looped),
        in_specs=[smem, hbm, hbm, hbm, hbm],
        out_specs=[hbm, smem],
        out_shape=[jax.ShapeDtypeStruct((n, width), bf16) for n in PARTS] + [jax.ShapeDtypeStruct((1,), f32)],
        scratch_shapes=[
            pltpu.VMEM((4, width, width), bf16),
            pltpu.VMEM((4, width, width), bf16),
            pltpu.VMEM((4, width, width), bf16),
            pltpu.VMEM((images, seq, width), bf16),
            pltpu.VMEM((images, seq, width), bf16),
            pltpu.VMEM((4, rows, width), bf16),
            pltpu.VMEM((4, rows, width), bf16),
            pltpu.SemaphoreType.DMA((6,)),
            pltpu.SemaphoreType.DMA((4,)),
            pltpu.SemaphoreType.DMA((4,)),
        ],
        name="gradient",
    )(ids, tok, cot, w, res)


def streamed(formula, sources, count, block=256):
    rows, width = sources[0].shape
    steps, inputs, total = rows // block, len(sources), len(sources) + count

    def kernel(*refs):
        hbm, vmem, sems = refs[:total], refs[total : 2 * total], refs[2 * total]

        def copy(j, i):
            here = pl.ds(i * block, block)
            ends = (hbm[j].at[here], vmem[j].at[here])
            return pltpu.make_async_copy(*(ends if j < inputs else ends[::-1]), sems.at[j, i])

        @pl.loop(0, steps)
        def _(i):
            for j in range(inputs):
                copy(j, i).start()

        @pl.loop(0, steps)
        def _(i):
            for j in range(inputs):
                copy(j, i).wait()

            @pl.loop(0, block // 32)
            def _(k):
                here = pl.ds(pl.multiple_of(i * block + k * 32, 32), 32)
                for j, part in enumerate(formula(*(v[here] for v in vmem[:inputs]))):
                    vmem[inputs + j][here] = part

            for j in range(inputs, total):
                copy(j, i).start()

        @pl.loop(0, steps)
        def _(i):
            for j in range(inputs, total):
                copy(j, i).wait()

    return pl.pallas_call(
        kernel,
        in_specs=[pl.BlockSpec(memory_space=pl.ANY)] * inputs,
        out_specs=[pl.BlockSpec(memory_space=pl.ANY)] * count,
        out_shape=[jax.ShapeDtypeStruct((rows, width), bf16)] * count,
        scratch_shapes=[pltpu.VMEM((rows, width), bf16)] * total + [pltpu.SemaphoreType.DMA((total, steps))],
        name="streamed",
    )(*sources)


def copied(sources, sizes):
    width, rows = sources[0].shape[1], sum(sizes)

    def places(heights):
        return [(side, row) for side, n in enumerate(heights) for row in range(n)]

    begin, end = places([s.shape[0] for s in sources]), places(sizes)
    cuts = sorted({0, rows, *range(0, rows, 512)} | {r for r in range(rows) if 0 in (begin[r][1], end[r][1])})
    moves = [(begin[r], end[r], r, n - r) for r, n in zip(cuts, cuts[1:])]

    def kernel(*refs):
        inputs, outs, (held, loaded, stored) = refs[: len(sources)], refs[len(sources) : -3], refs[-3:]
        loads, stores = [], []
        for j, ((s, i), (d, o), r, n) in enumerate(moves):
            here = held.at[pl.ds(r, n)]
            loads.append(pltpu.make_async_copy(inputs[s].at[pl.ds(i, n)], here, loaded.at[j]))
            stores.append(pltpu.make_async_copy(here, outs[d].at[pl.ds(o, n)], stored.at[j]))
        for load in loads:
            load.start()
        for load, store in zip(loads, stores):
            load.wait()
            store.start()
        for store in stores:
            store.wait()

    return pl.pallas_call(
        kernel,
        in_specs=[pl.BlockSpec(memory_space=pl.ANY)] * len(sources),
        out_specs=[pl.BlockSpec(memory_space=pl.ANY)] * len(sizes),
        out_shape=[jax.ShapeDtypeStruct((n, width), bf16) for n in sizes],
        scratch_shapes=[pltpu.VMEM((rows, width), bf16)] + [pltpu.SemaphoreType.DMA((len(moves),))] * 2,
        name="copied",
    )(*sources)


def coordinates(i):
    at = []
    for size in reversed(SIZES):
        at.append(i % size)
        i //= size
    return at[::-1]


def node_at(at):
    i = 0
    for a, size in zip(at, SIZES):
        i = i * size + a % size
    return i


def shifted(i, axis, steps):
    at = coordinates(i)
    at[NODE.index(axis)] += steps
    return node_at(at)


def routed(x, target):
    return lax.ppermute(x, NODE, [(i, target(i)) for i in range(256)])


def ring_sum(v, axis):
    def step(_, carry):
        moving, total = carry
        moving = routed(moving, lambda i: shifted(i, axis, -1))
        return moving, total + moving

    return lax.fori_loop(1, SIZES[NODE.index(axis)], step, (v, v))[1]


def sum_over(v, axes):
    for axis in axes:
        v = lax.psum(v, axis)
    return v


def form_sent(tracked, near, weights):
    tracker = 0.5 * (tracked.astype(f32) + near.astype(f32))
    return ((weights.astype(f32) - step_rate * tracker).astype(bf16),)


def kept(tracked, near, residue):
    return ((residue.astype(f32) + 0.5 * (near.astype(f32) - tracked.astype(f32))).astype(bf16),)


def mixed(own_sent, sent):
    return ((0.5 * (own_sent.astype(f32) + sent.astype(f32))).astype(bf16),)


def both(tracked, near, weights, peer_weights, residue):
    (own_sent,), (sent,) = form_sent(tracked, near, weights), form_sent(near, tracked, peer_weights)
    return *mixed(own_sent, sent), *kept(tracked, near, residue)


def first_sum(level, v):
    if level > 5:
        return sum_over(v, ("y", "x", "core"))
    return ring_sum(v, "z") if level > 0 else lax.psum(v, "core")


def second_sum(level, v):
    if level > 5:
        return lax.psum(v, "z")
    if level > 2:
        return sum_over(v, ("y", "core", "x"))
    return sum_over(ring_sum(v, "x"), ("core", "y")) if level > 0 else sum_over(v, ("y", "x", "z"))


def flat(x):
    return x.reshape(-1, x.shape[-1])


def after(x, *others):
    return lax.optimization_barrier((x, *others))[0]


def bring(level, x):
    ahead = lambda i: (i + 2**level) % 256
    if level != 6:
        return routed(x, ahead), lambda v: v
    large, small = copied([x], (CUT, x.shape[0] - CUT))
    three_down = lambda i: shifted(i, "z", -3)
    hop = routed(small, three_down)
    near = routed(large, ahead)
    return (near, hop), lambda pair, v: copied([pair[0], routed(after(pair[1], v), three_down)], (x.shape[0],))[0]


def bring_tracked(level, tracked, squares):
    near, finish = bring(level, tracked)
    total = first_sum(level, squares)
    return (finish(near, total) if level == 6 else near), total


def bring_sent(level, own_sent, total, tracked, near, residue):
    sent, finish = bring(level, own_sent)
    (new_residue,) = streamed(kept, (tracked, near, residue), 1)
    if level == 6:
        sent = finish(sent, new_residue)
    total = second_sum(level, after(total, new_residue))
    return sent, new_residue, total


def round_of(level, ids, tok, cot, weights, residue):
    tracked, squares = gradient_call(ids, tok, cot, weights, residue)
    branches = range(LEVELS - 1)
    near, total = lax.switch(level, [partial(bring_tracked, k) for k in branches], tracked, squares)
    (own_sent,) = streamed(form_sent, (tracked, near, flat(weights)), 1)
    sent, new_residue, total = lax.switch(
        level, [partial(bring_sent, k) for k in branches], own_sent, total, tracked, near, flat(residue)
    )
    (new_weights,) = streamed(mixed, (own_sent, sent), 1)
    return new_weights, new_residue, total


def halfway_round(ids, tok, cot, weights, residue):
    ahead = lambda i: (i + 128) % 256
    peer_weights = routed(flat(weights), ahead)
    tracked, squares = gradient_call(ids, tok, cot, weights, residue, looped=True)
    near = routed(tracked, ahead)
    total = sum_over(squares, ("y", "x", "core", "z"))
    new_weights, new_residue = streamed(both, (tracked, near, flat(weights), peer_weights, flat(residue)), 2)
    return new_weights, new_residue, total


def per_device(round_index, sample_ids, token_pool, cotangent_pool, weights, residue):
    level = round_index[0] % LEVELS
    new_weights, new_residue, total = lax.cond(
        level == LEVELS - 1,
        halfway_round,
        partial(round_of, jnp.minimum(level, LEVELS - 2)),
        sample_ids[0],
        token_pool[0],
        cotangent_pool[0],
        weights[0],
        residue[0],
    )
    grad_rms = jnp.sqrt(total.reshape(()) / (256 * weights.size))
    return new_weights.reshape(weights.shape), new_residue.reshape(weights.shape), grad_rms


def solution(mesh):
    torus = Mesh(mesh.devices.reshape(SIZES), NODE)
    split = P(NODE, None, None, None)
    return jax.shard_map(
        per_device,
        mesh=torus,
        in_specs=(P(), P(NODE, None), split, split, split, split),
        out_specs=(split, split, P()),
        check_vma=False,
    )
```

profile of v0, /device:TPU:1, one launch (start us, length us, event | category | flops | bytes accessed | tf_op | source)
XLA Modules:
  0.0 127.5 jit_solution(6274599454010600785)
XLA Ops:
  1.3 124.5 %conditional.3 = (bf16[2048,512]{1,0:T(8,128)(2,1)}, f32[1]{0:T(128)}, bf16[1,4,512,512]{3,2,1,0:T(8,128)(2,1)}) conditional(s32[]{:T(128)} %convert_element_type.3, (s32[]{:T(128)}, s32[8]{0:T(128)}, bf16[4,64,512]{2,1,0:T(8,128)(2,1)}, bf16[4,64,512]{2,1,0:T(8,128)(2,1)}, bf16[4,512,512]{2,1,0:T(8,128)(2,1)}, ...), branch_computations={%region_0.50_spmd, %region_50.55_spmd} | conditional | flops 10 | bytes 39453428 | solution.py:363
  1.3 9.5 %gradient.2 = (bf16[2048,512]{1,0:T(8,128)(2,1)}, f32[1]{0:T(128)}) custom-call(s32[8]{0:T(128)} %get-tuple-element.313.ids, bf16[4,64,512]{2,1,0:T(8,128)(2,1)} %get-tuple-element.314.tok, bf16[4,64,512]{2,1,0:T(8,128)(2,1)} %get-tuple-element.315.cot, bf16[4,512,512]{2,1,0:T(8,128)(2,1)} %bitcast.31, bf16[4,512,512]{2,1,0:T(8,128)(2,1)} %bitcast.19), custom_call_target="tpu_custom_call" | custom-call | tf_op jit(solution)/shard_map/cond/branch_0_fun/gradient/pallas_call | solution.py:131
  10.8 54.9 %conditional = (bf16[2048,512]{1,0:T(8,128)(2,1)}, f32[1]{0:T(128)}) conditional(s32[]{:T(128)} %clamp.0, (bf16[2048,512]{1,0:T(8,128)(2,1)}, f32[1]{0:T(128)}) %gradient.2, (bf16[2048,512]{1,0:T(8,128)(2,1)}, f32[1]{0:T(128)}) %gradient.2, (bf16[2048,512]{1,0:T(8,128)(2,1)}, f32[1]{0:T(128)}) %gradient.2, ...), branch_computations={%region_1.2_spmd, %region_3.5_spmd, %region_6.8_spmd, %region_9.11... | conditional | flops 3 | bytes 18743512 | solution.py:342
  10.9 2.1 %collective-permute-start.22 = (bf16[2048,512]{1,0:T(8,128)(2,1)}, bf16[2048,512]{1,0:T(8,128)(2,1)}, u32[]{:S(2)}, u32[]{:S(2)}) collective-permute-start(bf16[2048,512]{1,0:T(8,128)(2,1)} %get-tuple-element.235), channel_id=1, source_target_pairs={{0,8},{1,9},{2,10},{3,11},{4,12},{5,13},{6,14},{7,15},{8,16},{9,17... | collective-permute-start | bytes 6291464 | tf_op jit(solution)/shard_map/cond/branch_0_fun/cond/branch_3_fun/ppermute | solution.py:255
  13.6 43.0 %while.79 = (s32[]{:T(128)}, f32[1]{0:T(128)}, f32[1]{0:T(128)}, s32[]{:T(128)}) while((s32[]{:T(128)}, f32[1]{0:T(128)}, f32[1]{0:T(128)}, s32[]{:T(128)}) %tuple.176), condition=%wide.region_11.10_spmd, body=%wide.region_10.9_spmd.sunk | while | flops 3 | bytes 129 | solution.py:264
  13.6 5.7 %collective-permute-start.21 = (f32[1]{0:T(128)}, f32[1]{0:T(128)}, u32[]{:S(2)}, u32[]{:S(2)}) collective-permute-start(f32[1]{0:T(128)} %get-tuple-element.574), channel_id=1, source_target_pairs={{0,224},{1,225},{2,226},{3,227},{4,228},{5,229},{6,230},{7,231},{8... | collective-permute-start | bytes 20 | tf_op jit(solution)/shard_map/cond/branch_0_fun/cond/branch_3_fun/while/body/eval_jaxpr/ppermute | solution.py:255
  19.2 0.8 collective-permute-done.21
  21.8 2.9 %collective-permute-start.21 = (f32[1]{0:T(128)}, f32[1]{0:T(128)}, u32[]{:S(2)}, u32[]{:S(2)}) collective-permute-start(f32[1]{0:T(128)} %get-tuple-element.574), channel_id=1, source_target_pairs={{0,224},{1,225},{2,226},{3,227},{4,228},{5,229},{6,230},{7,231},{8... | collective-permute-start | bytes 20 | tf_op jit(solution)/shard_map/cond/branch_0_fun/cond/branch_3_fun/while/body/eval_jaxpr/ppermute | solution.py:255
  24.7 0.8 collective-permute-done.21
  27.2 3.3 %collective-permute-start.21 = (f32[1]{0:T(128)}, f32[1]{0:T(128)}, u32[]{:S(2)}, u32[]{:S(2)}) collective-permute-start(f32[1]{0:T(128)} %get-tuple-element.574), channel_id=1, source_target_pairs={{0,224},{1,225},{2,226},{3,227},{4,228},{5,229},{6,230},{7,231},{8... | collective-permute-start | bytes 20 | tf_op jit(solution)/shard_map/cond/branch_0_fun/cond/branch_3_fun/while/body/eval_jaxpr/ppermute | solution.py:255
  30.5 0.8 collective-permute-done.21
  33.1 3.3 %collective-permute-start.21 = (f32[1]{0:T(128)}, f32[1]{0:T(128)}, u32[]{:S(2)}, u32[]{:S(2)}) collective-permute-start(f32[1]{0:T(128)} %get-tuple-element.574), channel_id=1, source_target_pairs={{0,224},{1,225},{2,226},{3,227},{4,228},{5,229},{6,230},{7,231},{8... | collective-permute-start | bytes 20 | tf_op jit(solution)/shard_map/cond/branch_0_fun/cond/branch_3_fun/while/body/eval_jaxpr/ppermute | solution.py:255
  36.4 0.8 collective-permute-done.21
  39.0 3.3 %collective-permute-start.21 = (f32[1]{0:T(128)}, f32[1]{0:T(128)}, u32[]{:S(2)}, u32[]{:S(2)}) collective-permute-start(f32[1]{0:T(128)} %get-tuple-element.574), channel_id=1, source_target_pairs={{0,224},{1,225},{2,226},{3,227},{4,228},{5,229},{6,230},{7,231},{8... | collective-permute-start | bytes 20 | tf_op jit(solution)/shard_map/cond/branch_0_fun/cond/branch_3_fun/while/body/eval_jaxpr/ppermute | solution.py:255
  42.3 0.8 collective-permute-done.21
  44.8 3.3 %collective-permute-start.21 = (f32[1]{0:T(128)}, f32[1]{0:T(128)}, u32[]{:S(2)}, u32[]{:S(2)}) collective-permute-start(f32[1]{0:T(128)} %get-tuple-element.574), channel_id=1, source_target_pairs={{0,224},{1,225},{2,226},{3,227},{4,228},{5,229},{6,230},{7,231},{8... | collective-permute-start | bytes 20 | tf_op jit(solution)/shard_map/cond/branch_0_fun/cond/branch_3_fun/while/body/eval_jaxpr/ppermute | solution.py:255
  48.1 0.8 collective-permute-done.21
  50.7 3.3 %collective-permute-start.21 = (f32[1]{0:T(128)}, f32[1]{0:T(128)}, u32[]{:S(2)}, u32[]{:S(2)}) collective-permute-start(f32[1]{0:T(128)} %get-tuple-element.574), channel_id=1, source_target_pairs={{0,224},{1,225},{2,226},{3,227},{4,228},{5,229},{6,230},{7,231},{8... | collective-permute-start | bytes 20 | tf_op jit(solution)/shard_map/cond/branch_0_fun/cond/branch_3_fun/while/body/eval_jaxpr/ppermute | solution.py:255
  54.0 0.8 collective-permute-done.21
  56.6 8.6 %collective-permute-done.22 = bf16[2048,512]{1,0:T(8,128)(2,1)} collective-permute-done((bf16[2048,512]{1,0:T(8,128)(2,1)}, bf16[2048,512]{1,0:T(8,128)(2,1)}, u32[]{:S(2)}, u32[]{:S(2)}) %collective-permute-start.22) | collective-permute-done | bytes 2097184 | tf_op jit(solution)/shard_map/cond/branch_0_fun/cond/branch_3_fun/ppermute | solution.py:255
  65.7 0.0 copy-start
  65.7 4.4 %streamed.17.refs_0_ = bf16[2048,512]{1,0:T(8,128)(2,1)} custom-call(bf16[2048,512]{1,0:T(8,128)(2,1)} %get-tuple-element.318.refs_0_, bf16[2048,512]{1,0:T(8,128)(2,1)} %get-tuple-element.319.refs_1_, bf16[2048,512]{1,0:T(8,128)(2,1)} %bitcast.32), custom_call_target="tpu_custom_call" | custom-call | tf_op jit(solution)/shard_map/cond/branch_0_fun/streamed/pallas_call | solution.py:188
  70.2 0.0 copy-done
  70.2 52.0 %conditional.1 = (bf16[2048,512]{1,0:T(8,128)(2,1)}, bf16[2048,512]{1,0:T(8,128)(2,1)}, f32[1]{0:T(128)}) conditional(s32[]{:T(128)} %clamp.0, (bf16[2048,512]{1,0:T(8,128)(2,1)}, bf16[2048,512]{1,0:T(8,128)(2,1)}, bf16[2048,512]{1,0:T(8,128)(2,1)}, bf16[2048,512]{1,0:T(8,128)(2,1)S(1)}, f32[1]{0:T(128)}) %tuple.203, ...), branch_computations={%region_22.25_spmd, %region_26.30_spmd, %region_31.35_spmd, %regio... | conditional | flops 5 | bytes 12320948 | solution.py:344
  70.2 0.1 collective-permute-start.5
  70.3 3.4 %streamed.13 = bf16[2048,512]{1,0:T(8,128)(2,1)} custom-call(bf16[2048,512]{1,0:T(8,128)(2,1)} %get-tuple-element.286.refs_0_, bf16[2048,512]{1,0:T(8,128)(2,1)} %get-tuple-element.287.refs_1_, bf16[2048,512]{1,0:T(8,128)(2,1)S(1)} %get-tuple-element.288.refs_2_), custom_call_target="tpu_custom_call" | custom-call | tf_op jit(solution)/shard_map/cond/branch_0_fun/cond/branch_3_fun/streamed/pallas_call | solution.py:188
  73.7 10.1 %psum.161 = f32[1]{0:T(128)} all-reduce(f32[1]{0:T(128)} %get-tuple-element.290), channel_id=1, replica_groups=mesh['z'=8,'x'=4,'y'=4,'core'=2] {'y'}, use_global_device_ids=true, to_apply=%region_37.36 | all-reduce | flops 1 | bytes 8 | tf_op jit(solution)/shard_map/cond/branch_0_fun/cond/branch_3_fun/psum | solution.py:269
  83.8 5.3 %psum.162 = f32[1]{0:T(128)} all-reduce(f32[1]{0:T(128)} %psum.161), channel_id=1, replica_groups=mesh['z'=8,'x'=4,'y'=4,'core'=2] {'core'}, use_global_device_ids=true, to_apply=%region_38.37 | all-reduce | flops 1 | bytes 8 | tf_op jit(solution)/shard_map/cond/branch_0_fun/cond/branch_3_fun/psum | solution.py:269
  89.1 33.1 %psum.163 = f32[1]{0:T(128)} all-reduce(f32[1]{0:T(128)} %psum.162), channel_id=1, replica_groups=mesh['z'=8,'x'=4,'y'=4,'core'=2] {'x'}, use_global_device_ids=true, to_apply=%region_39.38 | all-reduce | flops 1 | bytes 8 | tf_op jit(solution)/shard_map/cond/branch_0_fun/cond/branch_3_fun/psum | solution.py:269
  122.2 0.0 collective-permute-done.5
  122.2 3.3 %streamed.18 = bf16[2048,512]{1,0:T(8,128)(2,1)} custom-call(bf16[2048,512]{1,0:T(8,128)(2,1)} %streamed.17.refs_0_, bf16[2048,512]{1,0:T(8,128)(2,1)} %get-tuple-element.325.refs_1_), custom_call_target="tpu_custom_call" | custom-call | tf_op jit(solution)/shard_map/cond/branch_0_fun/streamed/pallas_call | solution.py:188
Async XLA Ops:
  10.9 54.3 %collective-permute-start.22 = (bf16[2048,512]{1,0:T(8,128)(2,1)}, bf16[2048,512]{1,0:T(8,128)(2,1)}, u32[]{:S(2)}, u32[]{:S(2)}) collective-permute-start(bf16[2048,512]{1,0:T(8,128)(2,1)} %get-tuple-element.235), channel_id=1, source_target_pairs={{0,8},{1,9},{2,10},{3,11},{4,12},{5,13},{6,14},{7,15},{8,16},{9,17... | collective-permute-start | bytes 6291464 | tf_op jit(solution)/shard_map/cond/branch_0_fun/cond/branch_3_fun/ppermute | solution.py:255
  13.6 6.4 %collective-permute-start.21 = (f32[1]{0:T(128)}, f32[1]{0:T(128)}, u32[]{:S(2)}, u32[]{:S(2)}) collective-permute-start(f32[1]{0:T(128)} %get-tuple-element.574), channel_id=1, source_target_pairs={{0,224},{1,225},{2,226},{3,227},{4,228},{5,229},{6,230},{7,231},{8... | collective-permute-start | bytes 20 | tf_op jit(solution)/shard_map/cond/branch_0_fun/cond/branch_3_fun/while/body/eval_jaxpr/ppermute | solution.py:255
  21.8 3.6 %collective-permute-start.21 = (f32[1]{0:T(128)}, f32[1]{0:T(128)}, u32[]{:S(2)}, u32[]{:S(2)}) collective-permute-start(f32[1]{0:T(128)} %get-tuple-element.574), channel_id=1, source_target_pairs={{0,224},{1,225},{2,226},{3,227},{4,228},{5,229},{6,230},{7,231},{8... | collective-permute-start | bytes 20 | tf_op jit(solution)/shard_map/cond/branch_0_fun/cond/branch_3_fun/while/body/eval_jaxpr/ppermute | solution.py:255
  27.2 4.1 %collective-permute-start.21 = (f32[1]{0:T(128)}, f32[1]{0:T(128)}, u32[]{:S(2)}, u32[]{:S(2)}) collective-permute-start(f32[1]{0:T(128)} %get-tuple-element.574), channel_id=1, source_target_pairs={{0,224},{1,225},{2,226},{3,227},{4,228},{5,229},{6,230},{7,231},{8... | collective-permute-start | bytes 20 | tf_op jit(solution)/shard_map/cond/branch_0_fun/cond/branch_3_fun/while/body/eval_jaxpr/ppermute | solution.py:255
  33.1 4.1 %collective-permute-start.21 = (f32[1]{0:T(128)}, f32[1]{0:T(128)}, u32[]{:S(2)}, u32[]{:S(2)}) collective-permute-start(f32[1]{0:T(128)} %get-tuple-element.574), channel_id=1, source_target_pairs={{0,224},{1,225},{2,226},{3,227},{4,228},{5,229},{6,230},{7,231},{8... | collective-permute-start | bytes 20 | tf_op jit(solution)/shard_map/cond/branch_0_fun/cond/branch_3_fun/while/body/eval_jaxpr/ppermute | solution.py:255
  39.0 4.1 %collective-permute-start.21 = (f32[1]{0:T(128)}, f32[1]{0:T(128)}, u32[]{:S(2)}, u32[]{:S(2)}) collective-permute-start(f32[1]{0:T(128)} %get-tuple-element.574), channel_id=1, source_target_pairs={{0,224},{1,225},{2,226},{3,227},{4,228},{5,229},{6,230},{7,231},{8... | collective-permute-start | bytes 20 | tf_op jit(solution)/shard_map/cond/branch_0_fun/cond/branch_3_fun/while/body/eval_jaxpr/ppermute | solution.py:255
  44.8 4.1 %collective-permute-start.21 = (f32[1]{0:T(128)}, f32[1]{0:T(128)}, u32[]{:S(2)}, u32[]{:S(2)}) collective-permute-start(f32[1]{0:T(128)} %get-tuple-element.574), channel_id=1, source_target_pairs={{0,224},{1,225},{2,226},{3,227},{4,228},{5,229},{6,230},{7,231},{8... | collective-permute-start | bytes 20 | tf_op jit(solution)/shard_map/cond/branch_0_fun/cond/branch_3_fun/while/body/eval_jaxpr/ppermute | solution.py:255
  50.7 4.1 %collective-permute-start.21 = (f32[1]{0:T(128)}, f32[1]{0:T(128)}, u32[]{:S(2)}, u32[]{:S(2)}) collective-permute-start(f32[1]{0:T(128)} %get-tuple-element.574), channel_id=1, source_target_pairs={{0,224},{1,225},{2,226},{3,227},{4,228},{5,229},{6,230},{7,231},{8... | collective-permute-start | bytes 20 | tf_op jit(solution)/shard_map/cond/branch_0_fun/cond/branch_3_fun/while/body/eval_jaxpr/ppermute | solution.py:255
  65.7 4.5 %copy-start = (bf16[1,4,512,512]{3,2,1,0:T(8,128)(2,1)S(1)}, bf16[1,4,512,512]{3,2,1,0:T(8,128)(2,1)}, u32[]{:S(2)}) copy-start(bf16[1,4,512,512]{3,2,1,0:T(8,128)(2,1)} %get-tuple-element.321) | copy-start | bytes 6291460 | tf_op jit(solution)/shard_map/cond
  70.2 52.0 %collective-permute-start.5 = (bf16[2048,512]{1,0:T(8,128)(2,1)}, bf16[2048,512]{1,0:T(8,128)(2,1)}, u32[]{:S(2)}, u32[]{:S(2)}) collective-permute-start(bf16[2048,512]{1,0:T(8,128)(2,1)} %get-tuple-element.285), channel_id=1, source_target_pairs={{0,8},{1,9},{2,10},{3,11},{4,12},{5,13},{6,14},{7,15},{8,16},{9,17... | collective-permute-start | bytes 6291464 | tf_op jit(solution)/shard_map/cond/branch_0_fun/cond/branch_3_fun/ppermute | solution.py:255
where the time goes:
time: 128 us
  blocking collectives  48.4 us (38%)
  starting transfers between devices  27.3 us (21%)
  Pallas kernels  20.7 us (16%)
  waiting for transfers between devices  14.1 us (11%)
  loops' own time  14 us (11%)
  between operations  3.04 us (2%)
    psum x3, blocking collectives, sum_over(): v = lax.psum(v, axis)  48.4 us
    ppermute x9, starting transfers between devices, routed(): return lax.ppermute(x, NODE, [(i, target(i)) for i in range(256)])  27.3 us
    ppermute x9, waiting for transfers between devices, routed(): return lax.ppermute(x, NODE, [(i, target(i)) for i in range(256)])  14.1 us
    another operation x1, loops' own time, ring_sum(): return lax.fori_loop(1, SIZES[NODE.index(axis)], step, (v, v))[1]  12.5 us
    pallas_call x3, Pallas kernels, streamed(): pl.pallas_call(kernel, in_specs=[pl.BlockSpec(memory_space=pl.ANY)] * inp...  11.2 us
    pallas_call x1, Pallas kernels, gradient_call(): pl.pallas_call(partial(gradient_kernel, looped), in_specs=[smem, hbm, hbm...  9.53 us
  transfers between devices with their start and end apart: 9, of which 8 were waited for; matrix products, arithmetic and copies ran while one was open for 0% of the time, Pallas kernels for 3%

commit v1 on v0

--- a/solution.py
+++ b/solution.py
@@ -149,7 +149,7 @@
     )(ids, tok, cot, w, res)
 
 
-def streamed(formula, sources, count, block=256):
+def streamed(formula, sources, count, unit=128, block=256):
     rows, width = sources[0].shape
     steps, inputs, total = rows // block, len(sources), len(sources) + count
 
@@ -171,9 +171,9 @@
             for j in range(inputs):
                 copy(j, i).wait()
 
-            @pl.loop(0, block // 32)
+            @pl.loop(0, block // unit)
             def _(k):
-                here = pl.ds(pl.multiple_of(i * block + k * 32, 32), 32)
+                here = pl.ds(pl.multiple_of(i * block + k * unit, unit), unit)
                 for j, part in enumerate(formula(*(v[here] for v in vmem[:inputs]))):
                     vmem[inputs + j][here] = part
 
@@ -291,7 +291,7 @@
 def first_sum(level, v):
     if level > 5:
         return sum_over(v, ("y", "x", "core"))
-    return ring_sum(v, "z") if level > 0 else lax.psum(v, "core")
+    return ring_sum(v, "z") if level > 0 else lax.psum(ring_sum(v, "x"), "core")
 
 
 def second_sum(level, v):
@@ -299,7 +299,7 @@
         return lax.psum(v, "z")
     if level > 2:
         return sum_over(v, ("y", "core", "x"))
-    return sum_over(ring_sum(v, "x"), ("core", "y")) if level > 0 else sum_over(v, ("y", "x", "z"))
+    return sum_over(ring_sum(v, "x"), ("core", "y")) if level > 0 else sum_over(v, ("y", "z"))
 
 
 def flat(x):
@@ -329,7 +329,7 @@
 
 def bring_sent(level, own_sent, total, tracked, near, residue):
     sent, finish = bring(level, own_sent)
-    (new_residue,) = streamed(kept, (tracked, near, residue), 1)
+    (new_residue,) = streamed(kept, (tracked, near, residue), 1, 32)
     if level == 6:
         sent = finish(sent, new_residue)
     total = second_sum(level, after(total, new_residue))

time: 128 us -> 128 us (level)
  no operation moved by 1% of the time
where the time goes in v1:
time: 128 us
  blocking collectives  48.4 us (38%)
  starting transfers between devices  27.4 us (21%)
  Pallas kernels  20.8 us (16%)
  loops' own time  14.9 us (12%)
  waiting for transfers between devices  13 us (10%)
  between operations  3.04 us (2%)
    psum x3, blocking collectives, sum_over(): v = lax.psum(v, axis)  48.4 us
    ppermute x9, starting transfers between devices, routed(): return lax.ppermute(x, NODE, [(i, target(i)) for i in range(256)])  27.4 us
    another operation x1, loops' own time, ring_sum(): return lax.fori_loop(1, SIZES[NODE.index(axis)], step, (v, v))[1]  13.4 us
    ppermute x9, waiting for transfers between devices, routed(): return lax.ppermute(x, NODE, [(i, target(i)) for i in range(256)])  13 us
    pallas_call x3, Pallas kernels, streamed(): pl.pallas_call(kernel, in_specs=[pl.BlockSpec(memory_space=pl.ANY)] * inp...  11.2 us
    pallas_call x1, Pallas kernels, gradient_call(): pl.pallas_call(partial(gradient_kernel, looped), in_specs=[smem, hbm, hbm...  9.53 us
  transfers between devices with their start and end apart: 9, of which 8 were waited for; matrix products, arithmetic and copies ran while one was open for 0% of the time, Pallas kernels for 3%

profile of v1, /device:TPU:1, one launch (start us, length us, event | category | flops | bytes accessed | tf_op | source)
XLA Modules:
  0.0 127.6 jit_solution(13936911306903993830)
XLA Ops:
  1.3 124.5 %conditional.3 = (bf16[2048,512]{1,0:T(8,128)(2,1)}, f32[1]{0:T(128)}, bf16[1,4,512,512]{3,2,1,0:T(8,128)(2,1)}) conditional(s32[]{:T(128)} %convert_element_type.3, (s32[]{:T(128)}, s32[8]{0:T(128)}, bf16[4,64,512]{2,1,0:T(8,128)(2,1)}, bf16[4,64,512]{2,1,0:T(8,128)(2,1)}, bf16[4,512,512]{2,1,0:T(8,128)(2,1)}, ...), branch_computations={%region_0.51_spmd, %region_51.56_spmd} | conditional | flops 11 | bytes 39453428 | solution.py:363
  1.3 9.5 %gradient.2 = (bf16[2048,512]{1,0:T(8,128)(2,1)}, f32[1]{0:T(128)}) custom-call(s32[8]{0:T(128)} %get-tuple-element.330.ids, bf16[4,64,512]{2,1,0:T(8,128)(2,1)} %get-tuple-element.331.tok, bf16[4,64,512]{2,1,0:T(8,128)(2,1)} %get-tuple-element.332.cot, bf16[4,512,512]{2,1,0:T(8,128)(2,1)} %bitcast.31, bf16[4,512,512]{2,1,0:T(8,128)(2,1)} %bitcast.19), custom_call_target="tpu_custom_call" | custom-call | tf_op jit(solution)/shard_map/cond/branch_0_fun/gradient/pallas_call | solution.py:131
  10.8 54.9 %conditional = (bf16[2048,512]{1,0:T(8,128)(2,1)}, f32[1]{0:T(128)}) conditional(s32[]{:T(128)} %clamp.0, (bf16[2048,512]{1,0:T(8,128)(2,1)}, f32[1]{0:T(128)}) %gradient.2, (bf16[2048,512]{1,0:T(8,128)(2,1)}, f32[1]{0:T(128)}) %gradient.2, (bf16[2048,512]{1,0:T(8,128)(2,1)}, f32[1]{0:T(128)}) %gradient.2, ...), branch_computations={%region_1.4_spmd, %region_5.7_spmd, %region_8.10_spmd, %region_11.... | conditional | flops 4 | bytes 18743512 | solution.py:342
  10.9 2.1 %collective-permute-start.21 = (bf16[2048,512]{1,0:T(8,128)(2,1)}, bf16[2048,512]{1,0:T(8,128)(2,1)}, u32[]{:S(2)}, u32[]{:S(2)}) collective-permute-start(bf16[2048,512]{1,0:T(8,128)(2,1)} %get-tuple-element.252), channel_id=1, source_target_pairs={{0,8},{1,9},{2,10},{3,11},{4,12},{5,13},{6,14},{7,15},{8,16},{9,17... | collective-permute-start | bytes 6291464 | tf_op jit(solution)/shard_map/cond/branch_0_fun/cond/branch_3_fun/ppermute | solution.py:255
  13.6 44.1 %while.91 = (s32[]{:T(128)}, f32[1]{0:T(128)}, f32[1]{0:T(128)}, s32[]{:T(128)}) while((s32[]{:T(128)}, f32[1]{0:T(128)}, f32[1]{0:T(128)}, s32[]{:T(128)}) %tuple.188), condition=%wide.region_13.12_spmd, body=%wide.region_12.11_spmd.sunk | while | flops 3 | bytes 129 | solution.py:264
  13.6 5.7 %collective-permute-start.20 = (f32[1]{0:T(128)}, f32[1]{0:T(128)}, u32[]{:S(2)}, u32[]{:S(2)}) collective-permute-start(f32[1]{0:T(128)} %get-tuple-element.616), channel_id=1, source_target_pairs={{0,224},{1,225},{2,226},{3,227},{4,228},{5,229},{6,230},{7,231},{8... | collective-permute-start | bytes 20 | tf_op jit(solution)/shard_map/cond/branch_0_fun/cond/branch_3_fun/while/body/eval_jaxpr/ppermute | solution.py:255
  19.3 0.8 collective-permute-done.20
  22.0 3.0 %collective-permute-start.20 = (f32[1]{0:T(128)}, f32[1]{0:T(128)}, u32[]{:S(2)}, u32[]{:S(2)}) collective-permute-start(f32[1]{0:T(128)} %get-tuple-element.616), channel_id=1, source_target_pairs={{0,224},{1,225},{2,226},{3,227},{4,228},{5,229},{6,230},{7,231},{8... | collective-permute-start | bytes 20 | tf_op jit(solution)/shard_map/cond/branch_0_fun/cond/branch_3_fun/while/body/eval_jaxpr/ppermute | solution.py:255
  25.0 0.8 collective-permute-done.20
  27.7 3.3 %collective-permute-start.20 = (f32[1]{0:T(128)}, f32[1]{0:T(128)}, u32[]{:S(2)}, u32[]{:S(2)}) collective-permute-start(f32[1]{0:T(128)} %get-tuple-element.616), channel_id=1, source_target_pairs={{0,224},{1,225},{2,226},{3,227},{4,228},{5,229},{6,230},{7,231},{8... | collective-permute-start | bytes 20 | tf_op jit(solution)/shard_map/cond/branch_0_fun/cond/branch_3_fun/while/body/eval_jaxpr/ppermute | solution.py:255
  31.0 0.8 collective-permute-done.20
  33.7 3.3 %collective-permute-start.20 = (f32[1]{0:T(128)}, f32[1]{0:T(128)}, u32[]{:S(2)}, u32[]{:S(2)}) collective-permute-start(f32[1]{0:T(128)} %get-tuple-element.616), channel_id=1, source_target_pairs={{0,224},{1,225},{2,226},{3,227},{4,228},{5,229},{6,230},{7,231},{8... | collective-permute-start | bytes 20 | tf_op jit(solution)/shard_map/cond/branch_0_fun/cond/branch_3_fun/while/body/eval_jaxpr/ppermute | solution.py:255
  37.0 0.8 collective-permute-done.20
  39.7 3.3 %collective-permute-start.20 = (f32[1]{0:T(128)}, f32[1]{0:T(128)}, u32[]{:S(2)}, u32[]{:S(2)}) collective-permute-start(f32[1]{0:T(128)} %get-tuple-element.616), channel_id=1, source_target_pairs={{0,224},{1,225},{2,226},{3,227},{4,228},{5,229},{6,230},{7,231},{8... | collective-permute-start | bytes 20 | tf_op jit(solution)/shard_map/cond/branch_0_fun/cond/branch_3_fun/while/body/eval_jaxpr/ppermute | solution.py:255
  43.0 0.8 collective-permute-done.20
  45.7 3.3 %collective-permute-start.20 = (f32[1]{0:T(128)}, f32[1]{0:T(128)}, u32[]{:S(2)}, u32[]{:S(2)}) collective-permute-start(f32[1]{0:T(128)} %get-tuple-element.616), channel_id=1, source_target_pairs={{0,224},{1,225},{2,226},{3,227},{4,228},{5,229},{6,230},{7,231},{8... | collective-permute-start | bytes 20 | tf_op jit(solution)/shard_map/cond/branch_0_fun/cond/branch_3_fun/while/body/eval_jaxpr/ppermute | solution.py:255
  49.0 0.8 collective-permute-done.20
  51.7 3.3 %collective-permute-start.20 = (f32[1]{0:T(128)}, f32[1]{0:T(128)}, u32[]{:S(2)}, u32[]{:S(2)}) collective-permute-start(f32[1]{0:T(128)} %get-tuple-element.616), channel_id=1, source_target_pairs={{0,224},{1,225},{2,226},{3,227},{4,228},{5,229},{6,230},{7,231},{8... | collective-permute-start | bytes 20 | tf_op jit(solution)/shard_map/cond/branch_0_fun/cond/branch_3_fun/while/body/eval_jaxpr/ppermute | solution.py:255
  55.0 0.8 collective-permute-done.20
  57.7 7.5 %collective-permute-done.21 = bf16[2048,512]{1,0:T(8,128)(2,1)} collective-permute-done((bf16[2048,512]{1,0:T(8,128)(2,1)}, bf16[2048,512]{1,0:T(8,128)(2,1)}, u32[]{:S(2)}, u32[]{:S(2)}) %collective-permute-start.21) | collective-permute-done | bytes 2097184 | tf_op jit(solution)/shard_map/cond/branch_0_fun/cond/branch_3_fun/ppermute | solution.py:255
  65.7 0.0 copy-start
  65.7 4.5 %streamed.17.refs_0_ = bf16[2048,512]{1,0:T(8,128)(2,1)} custom-call(bf16[2048,512]{1,0:T(8,128)(2,1)} %get-tuple-element.335.refs_0_, bf16[2048,512]{1,0:T(8,128)(2,1)} %get-tuple-element.336.refs_1_, bf16[2048,512]{1,0:T(8,128)(2,1)} %bitcast.32), custom_call_target="tpu_custom_call" | custom-call | tf_op jit(solution)/shard_map/cond/branch_0_fun/streamed/pallas_call | solution.py:188
  70.2 0.0 copy-done
  70.2 52.0 %conditional.1 = (bf16[2048,512]{1,0:T(8,128)(2,1)}, bf16[2048,512]{1,0:T(8,128)(2,1)}, f32[1]{0:T(128)}) conditional(s32[]{:T(128)} %clamp.0, (bf16[2048,512]{1,0:T(8,128)(2,1)}, bf16[2048,512]{1,0:T(8,128)(2,1)}, bf16[2048,512]{1,0:T(8,128)(2,1)}, bf16[2048,512]{1,0:T(8,128)(2,1)S(1)}, f32[1]{0:T(128)}) %tuple.218, ...), branch_computations={%region_24.26_spmd, %region_27.31_spmd, %region_32.36_spmd, %regio... | conditional | flops 5 | bytes 12320948 | solution.py:344
  70.3 0.1 collective-permute-start.4
  70.3 3.4 %streamed.13 = bf16[2048,512]{1,0:T(8,128)(2,1)} custom-call(bf16[2048,512]{1,0:T(8,128)(2,1)} %get-tuple-element.303.refs_0_, bf16[2048,512]{1,0:T(8,128)(2,1)} %get-tuple-element.304.refs_1_, bf16[2048,512]{1,0:T(8,128)(2,1)S(1)} %get-tuple-element.305.refs_2_), custom_call_target="tpu_custom_call" | custom-call | tf_op jit(solution)/shard_map/cond/branch_0_fun/cond/branch_3_fun/streamed/pallas_call | solution.py:188
  73.8 10.1 %psum.154 = f32[1]{0:T(128)} all-reduce(f32[1]{0:T(128)} %get-tuple-element.307), channel_id=1, replica_groups=mesh['z'=8,'x'=4,'y'=4,'core'=2] {'y'}, use_global_device_ids=true, to_apply=%region_38.37 | all-reduce | flops 1 | bytes 8 | tf_op jit(solution)/shard_map/cond/branch_0_fun/cond/branch_3_fun/psum | solution.py:269
  83.8 5.3 %psum.155 = f32[1]{0:T(128)} all-reduce(f32[1]{0:T(128)} %psum.154), channel_id=1, replica_groups=mesh['z'=8,'x'=4,'y'=4,'core'=2] {'core'}, use_global_device_ids=true, to_apply=%region_39.38 | all-reduce | flops 1 | bytes 8 | tf_op jit(solution)/shard_map/cond/branch_0_fun/cond/branch_3_fun/psum | solution.py:269
  89.1 33.1 %psum.156 = f32[1]{0:T(128)} all-reduce(f32[1]{0:T(128)} %psum.155), channel_id=1, replica_groups=mesh['z'=8,'x'=4,'y'=4,'core'=2] {'x'}, use_global_device_ids=true, to_apply=%region_40.39 | all-reduce | flops 1 | bytes 8 | tf_op jit(solution)/shard_map/cond/branch_0_fun/cond/branch_3_fun/psum | solution.py:269
  122.2 0.0 collective-permute-done.4
  122.2 3.3 %streamed.18 = bf16[2048,512]{1,0:T(8,128)(2,1)} custom-call(bf16[2048,512]{1,0:T(8,128)(2,1)} %streamed.17.refs_0_, bf16[2048,512]{1,0:T(8,128)(2,1)} %get-tuple-element.342.refs_1_), custom_call_target="tpu_custom_call" | custom-call | tf_op jit(solution)/shard_map/cond/branch_0_fun/streamed/pallas_call | solution.py:188
Async XLA Ops:
  10.9 54.3 %collective-permute-start.21 = (bf16[2048,512]{1,0:T(8,128)(2,1)}, bf16[2048,512]{1,0:T(8,128)(2,1)}, u32[]{:S(2)}, u32[]{:S(2)}) collective-permute-start(bf16[2048,512]{1,0:T(8,128)(2,1)} %get-tuple-element.252), channel_id=1, source_target_pairs={{0,8},{1,9},{2,10},{3,11},{4,12},{5,13},{6,14},{7,15},{8,16},{9,17... | collective-permute-start | bytes 6291464 | tf_op jit(solution)/shard_map/cond/branch_0_fun/cond/branch_3_fun/ppermute | solution.py:255
  13.6 6.4 %collective-permute-start.20 = (f32[1]{0:T(128)}, f32[1]{0:T(128)}, u32[]{:S(2)}, u32[]{:S(2)}) collective-permute-start(f32[1]{0:T(128)} %get-tuple-element.616), channel_id=1, source_target_pairs={{0,224},{1,225},{2,226},{3,227},{4,228},{5,229},{6,230},{7,231},{8... | collective-permute-start | bytes 20 | tf_op jit(solution)/shard_map/cond/branch_0_fun/cond/branch_3_fun/while/body/eval_jaxpr/ppermute | solution.py:255
  22.0 3.8 %collective-permute-start.20 = (f32[1]{0:T(128)}, f32[1]{0:T(128)}, u32[]{:S(2)}, u32[]{:S(2)}) collective-permute-start(f32[1]{0:T(128)} %get-tuple-element.616), channel_id=1, source_target_pairs={{0,224},{1,225},{2,226},{3,227},{4,228},{5,229},{6,230},{7,231},{8... | collective-permute-start | bytes 20 | tf_op jit(solution)/shard_map/cond/branch_0_fun/cond/branch_3_fun/while/body/eval_jaxpr/ppermute | solution.py:255
  27.7 4.1 %collective-permute-start.20 = (f32[1]{0:T(128)}, f32[1]{0:T(128)}, u32[]{:S(2)}, u32[]{:S(2)}) collective-permute-start(f32[1]{0:T(128)} %get-tuple-element.616), channel_id=1, source_target_pairs={{0,224},{1,225},{2,226},{3,227},{4,228},{5,229},{6,230},{7,231},{8... | collective-permute-start | bytes 20 | tf_op jit(solution)/shard_map/cond/branch_0_fun/cond/branch_3_fun/while/body/eval_jaxpr/ppermute | solution.py:255
  33.7 4.1 %collective-permute-start.20 = (f32[1]{0:T(128)}, f32[1]{0:T(128)}, u32[]{:S(2)}, u32[]{:S(2)}) collective-permute-start(f32[1]{0:T(128)} %get-tuple-element.616), channel_id=1, source_target_pairs={{0,224},{1,225},{2,226},{3,227},{4,228},{5,229},{6,230},{7,231},{8... | collective-permute-start | bytes 20 | tf_op jit(solution)/shard_map/cond/branch_0_fun/cond/branch_3_fun/while/body/eval_jaxpr/ppermute | solution.py:255
  39.7 4.1 %collective-permute-start.20 = (f32[1]{0:T(128)}, f32[1]{0:T(128)}, u32[]{:S(2)}, u32[]{:S(2)}) collective-permute-start(f32[1]{0:T(128)} %get-tuple-element.616), channel_id=1, source_target_pairs={{0,224},{1,225},{2,226},{3,227},{4,228},{5,229},{6,230},{7,231},{8... | collective-permute-start | bytes 20 | tf_op jit(solution)/shard_map/cond/branch_0_fun/cond/branch_3_fun/while/body/eval_jaxpr/ppermute | solution.py:255
  45.7 4.1 %collective-permute-start.20 = (f32[1]{0:T(128)}, f32[1]{0:T(128)}, u32[]{:S(2)}, u32[]{:S(2)}) collective-permute-start(f32[1]{0:T(128)} %get-tuple-element.616), channel_id=1, source_target_pairs={{0,224},{1,225},{2,226},{3,227},{4,228},{5,229},{6,230},{7,231},{8... | collective-permute-start | bytes 20 | tf_op jit(solution)/shard_map/cond/branch_0_fun/cond/branch_3_fun/while/body/eval_jaxpr/ppermute | solution.py:255
  51.7 4.1 %collective-permute-start.20 = (f32[1]{0:T(128)}, f32[1]{0:T(128)}, u32[]{:S(2)}, u32[]{:S(2)}) collective-permute-start(f32[1]{0:T(128)} %get-tuple-element.616), channel_id=1, source_target_pairs={{0,224},{1,225},{2,226},{3,227},{4,228},{5,229},{6,230},{7,231},{8... | collective-permute-start | bytes 20 | tf_op jit(solution)/shard_map/cond/branch_0_fun/cond/branch_3_fun/while/body/eval_jaxpr/ppermute | solution.py:255
  65.7 4.5 %copy-start = (bf16[1,4,512,512]{3,2,1,0:T(8,128)(2,1)S(1)}, bf16[1,4,512,512]{3,2,1,0:T(8,128)(2,1)}, u32[]{:S(2)}) copy-start(bf16[1,4,512,512]{3,2,1,0:T(8,128)(2,1)} %get-tuple-element.338) | copy-start | bytes 6291460 | tf_op jit(solution)/shard_map/cond
  70.3 52.0 %collective-permute-start.4 = (bf16[2048,512]{1,0:T(8,128)(2,1)}, bf16[2048,512]{1,0:T(8,128)(2,1)}, u32[]{:S(2)}, u32[]{:S(2)}) collective-permute-start(bf16[2048,512]{1,0:T(8,128)(2,1)} %get-tuple-element.302), channel_id=1, source_target_pairs={{0,8},{1,9},{2,10},{3,11},{4,12},{5,13},{6,14},{7,15},{8,16},{9,17... | collective-permute-start | bytes 6291464 | tf_op jit(solution)/shard_map/cond/branch_0_fun/cond/branch_3_fun/ppermute | solution.py:255

commit v2 on v1

--- a/solution.py
+++ b/solution.py
@@ -298,8 +298,12 @@
     if level > 5:
         return lax.psum(v, "z")
     if level > 2:
-        return sum_over(v, ("y", "core", "x"))
-    return sum_over(ring_sum(v, "x"), ("core", "y")) if level > 0 else sum_over(v, ("y", "z"))
+        v = sum_over(v, ("y", "core"))
+        return ring_sum(v, "x") if level == 3 else lax.psum(v, "x")
+    if level == 0:
+        return sum_over(v, ("y", "z"))
+    v = lax.psum(ring_sum(v, "x"), "core")
+    return ring_sum(v, "y") if level == 1 else lax.psum(v, "y")
 
 
 def flat(x):

time: 128 us -> 127 us (level)
  blocking collectives: 48.4 us -> 15.4 us
  waiting for transfers between devices: 13 us -> 34.5 us
  loops' own time: 14.9 us -> 20 us
  starting transfers between devices: 27.4 us -> 32.1 us
    psum x3 -> x2, blocking collectives: 48.4 us -> 15.4 us  [sum_over(): v = lax.psum(v, axis)]
    ppermute x9 -> x12, waiting for transfers between devices: 13 us -> 34.5 us  [routed(): return lax.ppermute(x, NODE, [(i, target(i)) for i in range(256)])]
    ppermute x9 -> x12, starting transfers between devices: 27.4 us -> 32.1 us  [routed(): return lax.ppermute(x, NODE, [(i, target(i)) for i in range(256)])]
    another operation x1 -> x2, loops' own time: 13.4 us -> 17.2 us  [ring_sum(): return lax.fori_loop(1, SIZES[NODE.index(axis)], step, (v, v))[1]]
  transfers between devices with their start and end apart: 9 -> 12, of which waited for: 8 -> 12; matrix products, arithmetic and copies ran while one was open for 0% -> 0% of each run, Pallas kernels for 3% -> 3%
where the time goes in v2:
time: 127 us; the launch traced here: 126 us
  waiting for transfers between devices  34.5 us (27%)
  starting transfers between devices  32.1 us (25%)
  Pallas kernels  20.8 us (16%)
  loops' own time  20 us (16%)
  blocking collectives  15.4 us (12%)
  between operations  3.04 us (2%)
    ppermute x12, waiting for transfers between devices, routed(): return lax.ppermute(x, NODE, [(i, target(i)) for i in range(256)])  34.5 us
    ppermute x12, starting transfers between devices, routed(): return lax.ppermute(x, NODE, [(i, target(i)) for i in range(256)])  32.1 us
    another operation x2, loops' own time, ring_sum(): return lax.fori_loop(1, SIZES[NODE.index(axis)], step, (v, v))[1]  17.2 us
    psum x2, blocking collectives, sum_over(): v = lax.psum(v, axis)  15.4 us
    pallas_call x3, Pallas kernels, streamed(): pl.pallas_call(kernel, in_specs=[pl.BlockSpec(memory_space=pl.ANY)] * inp...  11.2 us
    pallas_call x1, Pallas kernels, gradient_call(): pl.pallas_call(partial(gradient_kernel, looped), in_specs=[smem, hbm, hbm...  9.53 us
  transfers between devices with their start and end apart: 12, of which 12 were waited for; matrix products, arithmetic and copies ran while one was open for 0% of the time, Pallas kernels for 3%

profile of v2, /device:TPU:1, one launch (start us, length us, event | category | flops | bytes accessed | tf_op | source)
XLA Modules:
  0.0 125.7 jit_solution(6583461329376110944)
XLA Ops:
  1.3 122.7 %conditional.3 = (bf16[2048,512]{1,0:T(8,128)(2,1)}, f32[1]{0:T(128)}, bf16[1,4,512,512]{3,2,1,0:T(8,128)(2,1)}) conditional(s32[]{:T(128)} %convert_element_type.3, (s32[]{:T(128)}, s32[8]{0:T(128)}, bf16[4,64,512]{2,1,0:T(8,128)(2,1)}, bf16[4,64,512]{2,1,0:T(8,128)(2,1)}, bf16[4,512,512]{2,1,0:T(8,128)(2,1)}, ...), branch_computations={%region_0.53_spmd, %region_53.58_spmd} | conditional | flops 13 | bytes 39453428 | solution.py:367
  1.3 9.5 %gradient.2 = (bf16[2048,512]{1,0:T(8,128)(2,1)}, f32[1]{0:T(128)}) custom-call(s32[8]{0:T(128)} %get-tuple-element.364.ids, bf16[4,64,512]{2,1,0:T(8,128)(2,1)} %get-tuple-element.365.tok, bf16[4,64,512]{2,1,0:T(8,128)(2,1)} %get-tuple-element.366.cot, bf16[4,512,512]{2,1,0:T(8,128)(2,1)} %bitcast.31, bf16[4,512,512]{2,1,0:T(8,128)(2,1)} %bitcast.19), custom_call_target="tpu_custom_call" | custom-call | tf_op jit(solution)/shard_map/cond/branch_0_fun/gradient/pallas_call | solution.py:131
  10.8 54.9 %conditional = (bf16[2048,512]{1,0:T(8,128)(2,1)}, f32[1]{0:T(128)}) conditional(s32[]{:T(128)} %clamp.0, (bf16[2048,512]{1,0:T(8,128)(2,1)}, f32[1]{0:T(128)}) %gradient.2, (bf16[2048,512]{1,0:T(8,128)(2,1)}, f32[1]{0:T(128)}) %gradient.2, (bf16[2048,512]{1,0:T(8,128)(2,1)}, f32[1]{0:T(128)}) %gradient.2, ...), branch_computations={%region_1.4_spmd, %region_5.7_spmd, %region_8.10_spmd, %region_11.... | conditional | flops 4 | bytes 18743512 | solution.py:346
  10.9 2.1 %collective-permute-start.23 = (bf16[2048,512]{1,0:T(8,128)(2,1)}, bf16[2048,512]{1,0:T(8,128)(2,1)}, u32[]{:S(2)}, u32[]{:S(2)}) collective-permute-start(bf16[2048,512]{1,0:T(8,128)(2,1)} %get-tuple-element.276), channel_id=1, source_target_pairs={{0,8},{1,9},{2,10},{3,11},{4,12},{5,13},{6,14},{7,15},{8,16},{9,17... | collective-permute-start | bytes 6291464 | tf_op jit(solution)/shard_map/cond/branch_0_fun/cond/branch_3_fun/ppermute | solution.py:255
  13.6 44.1 %while.113 = (s32[]{:T(128)}, f32[1]{0:T(128)}, f32[1]{0:T(128)}, s32[]{:T(128)}) while((s32[]{:T(128)}, f32[1]{0:T(128)}, f32[1]{0:T(128)}, s32[]{:T(128)}) %tuple.218), condition=%wide.region_13.12_spmd, body=%wide.region_12.11_spmd.sunk | while | flops 3 | bytes 129 | solution.py:264
  13.6 5.7 %collective-permute-start.22 = (f32[1]{0:T(128)}, f32[1]{0:T(128)}, u32[]{:S(2)}, u32[]{:S(2)}) collective-permute-start(f32[1]{0:T(128)} %get-tuple-element.724), channel_id=1, source_target_pairs={{0,224},{1,225},{2,226},{3,227},{4,228},{5,229},{6,230},{7,231},{8... | collective-permute-start | bytes 20 | tf_op jit(solution)/shard_map/cond/branch_0_fun/cond/branch_3_fun/while/body/eval_jaxpr/ppermute | solution.py:255
  19.3 0.8 collective-permute-done.22
  22.0 3.0 %collective-permute-start.22 = (f32[1]{0:T(128)}, f32[1]{0:T(128)}, u32[]{:S(2)}, u32[]{:S(2)}) collective-permute-start(f32[1]{0:T(128)} %get-tuple-element.724), channel_id=1, source_target_pairs={{0,224},{1,225},{2,226},{3,227},{4,228},{5,229},{6,230},{7,231},{8... | collective-permute-start | bytes 20 | tf_op jit(solution)/shard_map/cond/branch_0_fun/cond/branch_3_fun/while/body/eval_jaxpr/ppermute | solution.py:255
  25.0 0.8 collective-permute-done.22
  27.7 3.3 %collective-permute-start.22 = (f32[1]{0:T(128)}, f32[1]{0:T(128)}, u32[]{:S(2)}, u32[]{:S(2)}) collective-permute-start(f32[1]{0:T(128)} %get-tuple-element.724), channel_id=1, source_target_pairs={{0,224},{1,225},{2,226},{3,227},{4,228},{5,229},{6,230},{7,231},{8... | collective-permute-start | bytes 20 | tf_op jit(solution)/shard_map/cond/branch_0_fun/cond/branch_3_fun/while/body/eval_jaxpr/ppermute | solution.py:255
  31.0 0.8 collective-permute-done.22
  33.7 3.3 %collective-permute-start.22 = (f32[1]{0:T(128)}, f32[1]{0:T(128)}, u32[]{:S(2)}, u32[]{:S(2)}) collective-permute-start(f32[1]{0:T(128)} %get-tuple-element.724), channel_id=1, source_target_pairs={{0,224},{1,225},{2,226},{3,227},{4,228},{5,229},{6,230},{7,231},{8... | collective-permute-start | bytes 20 | tf_op jit(solution)/shard_map/cond/branch_0_fun/cond/branch_3_fun/while/body/eval_jaxpr/ppermute | solution.py:255
  39.7 3.3 %collective-permute-start.22 = (f32[1]{0:T(128)}, f32[1]{0:T(128)}, u32[]{:S(2)}, u32[]{:S(2)}) collective-permute-start(f32[1]{0:T(128)} %get-tuple-element.724), channel_id=1, source_target_pairs={{0,224},{1,225},{2,226},{3,227},{4,228},{5,229},{6,230},{7,231},{8... | collective-permute-start | bytes 20 | tf_op jit(solution)/shard_map/cond/branch_0_fun/cond/branch_3_fun/while/body/eval_jaxpr/ppermute | solution.py:255
  43.0 0.8 collective-permute-done.22
  45.7 3.3 %collective-permute-start.22 = (f32[1]{0:T(128)}, f32[1]{0:T(128)}, u32[]{:S(2)}, u32[]{:S(2)}) collective-permute-start(f32[1]{0:T(128)} %get-tuple-element.724), channel_id=1, source_target_pairs={{0,224},{1,225},{2,226},{3,227},{4,228},{5,229},{6,230},{7,231},{8... | collective-permute-start | bytes 20 | tf_op jit(solution)/shard_map/cond/branch_0_fun/cond/branch_3_fun/while/body/eval_jaxpr/ppermute | solution.py:255
  49.0 0.8 collective-permute-done.22
  51.7 3.3 %collective-permute-start.22 = (f32[1]{0:T(128)}, f32[1]{0:T(128)}, u32[]{:S(2)}, u32[]{:S(2)}) collective-permute-start(f32[1]{0:T(128)} %get-tuple-element.724), channel_id=1, source_target_pairs={{0,224},{1,225},{2,226},{3,227},{4,228},{5,229},{6,230},{7,231},{8... | collective-permute-start | bytes 20 | tf_op jit(solution)/shard_map/cond/branch_0_fun/cond/branch_3_fun/while/body/eval_jaxpr/ppermute | solution.py:255
  55.0 0.8 collective-permute-done.22
  57.7 7.5 %collective-permute-done.23 = bf16[2048,512]{1,0:T(8,128)(2,1)} collective-permute-done((bf16[2048,512]{1,0:T(8,128)(2,1)}, bf16[2048,512]{1,0:T(8,128)(2,1)}, u32[]{:S(2)}, u32[]{:S(2)}) %collective-permute-start.23) | collective-permute-done | bytes 2097184 | tf_op jit(solution)/shard_map/cond/branch_0_fun/cond/branch_3_fun/ppermute | solution.py:255
  65.7 4.5 %streamed.17.refs_0_ = bf16[2048,512]{1,0:T(8,128)(2,1)} custom-call(bf16[2048,512]{1,0:T(8,128)(2,1)} %get-tuple-element.369.refs_0_, bf16[2048,512]{1,0:T(8,128)(2,1)} %get-tuple-element.370.refs_1_, bf16[2048,512]{1,0:T(8,128)(2,1)} %bitcast.32), custom_call_target="tpu_custom_call" | custom-call | tf_op jit(solution)/shard_map/cond/branch_0_fun/streamed/pallas_call | solution.py:188
  70.2 50.2 %conditional.1 = (bf16[2048,512]{1,0:T(8,128)(2,1)}, bf16[2048,512]{1,0:T(8,128)(2,1)}, f32[1]{0:T(128)}) conditional(s32[]{:T(128)} %clamp.0, (bf16[2048,512]{1,0:T(8,128)(2,1)}, bf16[2048,512]{1,0:T(8,128)(2,1)}, bf16[2048,512]{1,0:T(8,128)(2,1)}, bf16[2048,512]{1,0:T(8,128)(2,1)S(1)}, f32[1]{0:T(128)}) %tuple.248, ...), branch_computations={%region_24.26_spmd, %region_27.32_spmd, %region_33.37_spmd, %regio... | conditional | flops 7 | bytes 12320948 | solution.py:348
  70.3 3.4 %streamed.13 = bf16[2048,512]{1,0:T(8,128)(2,1)} custom-call(bf16[2048,512]{1,0:T(8,128)(2,1)} %get-tuple-element.336.refs_0_, bf16[2048,512]{1,0:T(8,128)(2,1)} %get-tuple-element.337.refs_1_, bf16[2048,512]{1,0:T(8,128)(2,1)S(1)} %get-tuple-element.338.refs_2_), custom_call_target="tpu_custom_call" | custom-call | tf_op jit(solution)/shard_map/cond/branch_0_fun/cond/branch_3_fun/streamed/pallas_call | solution.py:188
  73.8 10.1 %psum.141 = f32[1]{0:T(128)} all-reduce(f32[1]{0:T(128)} %get-tuple-element.340), channel_id=1, replica_groups=mesh['z'=8,'x'=4,'y'=4,'core'=2] {'y'}, use_global_device_ids=true, to_apply=%region_39.38 | all-reduce | flops 1 | bytes 8 | tf_op jit(solution)/shard_map/cond/branch_0_fun/cond/branch_3_fun/psum | solution.py:269
  83.8 5.3 %psum.142 = f32[1]{0:T(128)} all-reduce(f32[1]{0:T(128)} %psum.141), channel_id=1, replica_groups=mesh['z'=8,'x'=4,'y'=4,'core'=2] {'core'}, use_global_device_ids=true, to_apply=%region_40.39 | all-reduce | flops 1 | bytes 8 | tf_op jit(solution)/shard_map/cond/branch_0_fun/cond/branch_3_fun/psum | solution.py:269
  89.8 12.5 %while.119 = (s32[]{:T(128)}, f32[1]{0:T(128)}, f32[1]{0:T(128)}, s32[]{:T(128)}) while((s32[]{:T(128)}, f32[1]{0:T(128)}, f32[1]{0:T(128)}, s32[]{:T(128)}) %tuple.200), condition=%wide.region_42.41_spmd, body=%wide.region_41.40_spmd.sunk | while | flops 3 | bytes 129 | solution.py:264
  90.4 0.8 collective-permute-start.11
  91.2 2.1 %collective-permute-done.11 = f32[1]{0:T(128)} collective-permute-done((f32[1]{0:T(128)}, f32[1]{0:T(128)}, u32[]{:S(2)}, u32[]{:S(2)}) %collective-permute-start.11) | collective-permute-done | bytes 36 | tf_op jit(solution)/shard_map/cond/branch_0_fun/cond/branch_3_fun/while/body/eval_jaxpr/ppermute | solution.py:255
  94.6 1.6 %collective-permute-start.11 = (f32[1]{0:T(128)}, f32[1]{0:T(128)}, u32[]{:S(2)}, u32[]{:S(2)}) collective-permute-start(f32[1]{0:T(128)} %copy.13), channel_id=1, source_target_pairs={{0,24},{1,25},{2,26},{3,27},{4,28},{5,29},{6,30},{7,31},{8,0},{9,1... | collective-permute-start | bytes 20 | tf_op jit(solution)/shard_map/cond/branch_0_fun/cond/branch_3_fun/while/body/eval_jaxpr/ppermute | solution.py:255
  96.2 1.3 %collective-permute-done.11 = f32[1]{0:T(128)} collective-permute-done((f32[1]{0:T(128)}, f32[1]{0:T(128)}, u32[]{:S(2)}, u32[]{:S(2)}) %collective-permute-start.11) | collective-permute-done | bytes 36 | tf_op jit(solution)/shard_map/cond/branch_0_fun/cond/branch_3_fun/while/body/eval_jaxpr/ppermute | solution.py:255
  98.8 2.3 %collective-permute-start.11 = (f32[1]{0:T(128)}, f32[1]{0:T(128)}, u32[]{:S(2)}, u32[]{:S(2)}) collective-permute-start(f32[1]{0:T(128)} %copy.13), channel_id=1, source_target_pairs={{0,24},{1,25},{2,26},{3,27},{4,28},{5,29},{6,30},{7,31},{8,0},{9,1... | collective-permute-start | bytes 20 | tf_op jit(solution)/shard_map/cond/branch_0_fun/cond/branch_3_fun/while/body/eval_jaxpr/ppermute | solution.py:255
  102.3 17.6 %collective-permute-done.12 = bf16[2048,512]{1,0:T(8,128)(2,1)} collective-permute-done((bf16[2048,512]{1,0:T(8,128)(2,1)}, bf16[2048,512]{1,0:T(8,128)(2,1)}, u32[]{:S(2)}, u32[]{:S(2)}) %collective-permute-start.12) | collective-permute-done | bytes 2097184 | tf_op jit(solution)/shard_map/cond/branch_0_fun/cond/branch_3_fun/ppermute | solution.py:255
  120.4 3.3 %streamed.18 = bf16[2048,512]{1,0:T(8,128)(2,1)} custom-call(bf16[2048,512]{1,0:T(8,128)(2,1)} %streamed.17.refs_0_, bf16[2048,512]{1,0:T(8,128)(2,1)} %get-tuple-element.376.refs_1_), custom_call_target="tpu_custom_call" | custom-call | tf_op jit(solution)/shard_map/cond/branch_0_fun/streamed/pallas_call | solution.py:188
  (5 shorter events, 1.4 us)
Async XLA Ops:
  10.9 54.3 %collective-permute-start.23 = (bf16[2048,512]{1,0:T(8,128)(2,1)}, bf16[2048,512]{1,0:T(8,128)(2,1)}, u32[]{:S(2)}, u32[]{:S(2)}) collective-permute-start(bf16[2048,512]{1,0:T(8,128)(2,1)} %get-tuple-element.276), channel_id=1, source_target_pairs={{0,8},{1,9},{2,10},{3,11},{4,12},{5,13},{6,14},{7,15},{8,16},{9,17... | collective-permute-start | bytes 6291464 | tf_op jit(solution)/shard_map/cond/branch_0_fun/cond/branch_3_fun/ppermute | solution.py:255
  13.6 6.4 %collective-permute-start.22 = (f32[1]{0:T(128)}, f32[1]{0:T(128)}, u32[]{:S(2)}, u32[]{:S(2)}) collective-permute-start(f32[1]{0:T(128)} %get-tuple-element.724), channel_id=1, source_target_pairs={{0,224},{1,225},{2,226},{3,227},{4,228},{5,229},{6,230},{7,231},{8... | collective-permute-start | bytes 20 | tf_op jit(solution)/shard_map/cond/branch_0_fun/cond/branch_3_fun/while/body/eval_jaxpr/ppermute | solution.py:255
  22.0 3.8 %collective-permute-start.22 = (f32[1]{0:T(128)}, f32[1]{0:T(128)}, u32[]{:S(2)}, u32[]{:S(2)}) collective-permute-start(f32[1]{0:T(128)} %get-tuple-element.724), channel_id=1, source_target_pairs={{0,224},{1,225},{2,226},{3,227},{4,228},{5,229},{6,230},{7,231},{8... | collective-permute-start | bytes 20 | tf_op jit(solution)/shard_map/cond/branch_0_fun/cond/branch_3_fun/while/body/eval_jaxpr/ppermute | solution.py:255
  27.7 4.1 %collective-permute-start.22 = (f32[1]{0:T(128)}, f32[1]{0:T(128)}, u32[]{:S(2)}, u32[]{:S(2)}) collective-permute-start(f32[1]{0:T(128)} %get-tuple-element.724), channel_id=1, source_target_pairs={{0,224},{1,225},{2,226},{3,227},{4,228},{5,229},{6,230},{7,231},{8... | collective-permute-start | bytes 20 | tf_op jit(solution)/shard_map/cond/branch_0_fun/cond/branch_3_fun/while/body/eval_jaxpr/ppermute | solution.py:255
  33.7 4.1 %collective-permute-start.22 = (f32[1]{0:T(128)}, f32[1]{0:T(128)}, u32[]{:S(2)}, u32[]{:S(2)}) collective-permute-start(f32[1]{0:T(128)} %get-tuple-element.724), channel_id=1, source_target_pairs={{0,224},{1,225},{2,226},{3,227},{4,228},{5,229},{6,230},{7,231},{8... | collective-permute-start | bytes 20 | tf_op jit(solution)/shard_map/cond/branch_0_fun/cond/branch_3_fun/while/body/eval_jaxpr/ppermute | solution.py:255
  39.7 4.1 %collective-permute-start.22 = (f32[1]{0:T(128)}, f32[1]{0:T(128)}, u32[]{:S(2)}, u32[]{:S(2)}) collective-permute-start(f32[1]{0:T(128)} %get-tuple-element.724), channel_id=1, source_target_pairs={{0,224},{1,225},{2,226},{3,227},{4,228},{5,229},{6,230},{7,231},{8... | collective-permute-start | bytes 20 | tf_op jit(solution)/shard_map/cond/branch_0_fun/cond/branch_3_fun/while/body/eval_jaxpr/ppermute | solution.py:255
  45.7 4.1 %collective-permute-start.22 = (f32[1]{0:T(128)}, f32[1]{0:T(128)}, u32[]{:S(2)}, u32[]{:S(2)}) collective-permute-start(f32[1]{0:T(128)} %get-tuple-element.724), channel_id=1, source_target_pairs={{0,224},{1,225},{2,226},{3,227},{4,228},{5,229},{6,230},{7,231},{8... | collective-permute-start | bytes 20 | tf_op jit(solution)/shard_map/cond/branch_0_fun/cond/branch_3_fun/while/body/eval_jaxpr/ppermute | solution.py:255
  51.7 4.1 %collective-permute-start.22 = (f32[1]{0:T(128)}, f32[1]{0:T(128)}, u32[]{:S(2)}, u32[]{:S(2)}) collective-permute-start(f32[1]{0:T(128)} %get-tuple-element.724), channel_id=1, source_target_pairs={{0,224},{1,225},{2,226},{3,227},{4,228},{5,229},{6,230},{7,231},{8... | collective-permute-start | bytes 20 | tf_op jit(solution)/shard_map/cond/branch_0_fun/cond/branch_3_fun/while/body/eval_jaxpr/ppermute | solution.py:255
  65.7 4.5 %copy-start = (bf16[1,4,512,512]{3,2,1,0:T(8,128)(2,1)S(1)}, bf16[1,4,512,512]{3,2,1,0:T(8,128)(2,1)}, u32[]{:S(2)}) copy-start(bf16[1,4,512,512]{3,2,1,0:T(8,128)(2,1)} %get-tuple-element.372) | copy-start | bytes 6291460 | tf_op jit(solution)/shard_map/cond
  70.3 49.6 %collective-permute-start.12 = (bf16[2048,512]{1,0:T(8,128)(2,1)}, bf16[2048,512]{1,0:T(8,128)(2,1)}, u32[]{:S(2)}, u32[]{:S(2)}) collective-permute-start(bf16[2048,512]{1,0:T(8,128)(2,1)} %get-tuple-element.335), channel_id=1, source_target_pairs={{0,8},{1,9},{2,10},{3,11},{4,12},{5,13},{6,14},{7,15},{8,16},{9,17... | collective-permute-start | bytes 6291464 | tf_op jit(solution)/shard_map/cond/branch_0_fun/cond/branch_3_fun/ppermute | solution.py:255
  90.4 2.9 %collective-permute-start.11 = (f32[1]{0:T(128)}, f32[1]{0:T(128)}, u32[]{:S(2)}, u32[]{:S(2)}) collective-permute-start(f32[1]{0:T(128)} %copy.13), channel_id=1, source_target_pairs={{0,24},{1,25},{2,26},{3,27},{4,28},{5,29},{6,30},{7,31},{8,0},{9,1... | collective-permute-start | bytes 20 | tf_op jit(solution)/shard_map/cond/branch_0_fun/cond/branch_3_fun/while/body/eval_jaxpr/ppermute | solution.py:255
  94.6 2.9 %collective-permute-start.11 = (f32[1]{0:T(128)}, f32[1]{0:T(128)}, u32[]{:S(2)}, u32[]{:S(2)}) collective-permute-start(f32[1]{0:T(128)} %copy.13), channel_id=1, source_target_pairs={{0,24},{1,25},{2,26},{3,27},{4,28},{5,29},{6,30},{7,31},{8,0},{9,1... | collective-permute-start | bytes 20 | tf_op jit(solution)/shard_map/cond/branch_0_fun/cond/branch_3_fun/while/body/eval_jaxpr/ppermute | solution.py:255
  98.8 2.9 %collective-permute-start.11 = (f32[1]{0:T(128)}, f32[1]{0:T(128)}, u32[]{:S(2)}, u32[]{:S(2)}) collective-permute-start(f32[1]{0:T(128)} %copy.13), channel_id=1, source_target_pairs={{0,24},{1,25},{2,26},{3,27},{4,28},{5,29},{6,30},{7,31},{8,0},{9,1... | collective-permute-start | bytes 20 | tf_op jit(solution)/shard_map/cond/branch_0_fun/cond/branch_3_fun/while/body/eval_jaxpr/ppermute | solution.py:255
